TPU v7x, 256 devices: a whole 4x4x8 slice. The times are simulated.
256 devices in a mesh: blk: 128 (over y, z, x_lo, core), rel: 2 (over x_hi).
Axes of the slice: x: 4 (x_hi: 2, x_lo: 2; x = x_hi * 2 + x_lo), y: 4, z: 8, core: 2. Of those that a mesh axis runs over, the one named last changes fastest.
Arguments:
- user_table: float32 [131072, 512], P(('blk', 'rel')), may hold values from -1.5 to 1.5
- user_accum: float32 [131072], P(('blk', 'rel')), may hold values from 1 to 100
- item_table: float32 [262144, 512], P(('blk', 'rel')), may hold values from -1.5 to 1.5
- item_accum: float32 [262144], P(('blk', 'rel')), may hold values from 1 to 100
- relation: bfloat16 [512, 512], replicated, may hold values from -0.25 to 0.25
- relation_accum: float32 [512], replicated, may hold values from 0.5 to 8
- targets: bfloat16 [2, 131072, 2048], P(None, 'blk', 'rel'), may hold values from 0 to 1
Outputs:
- user_table_next: float32 [131072, 512], P(('blk', 'rel'))
- user_accum_next: float32 [131072], P(('blk', 'rel'))
- item_table_next: float32 [262144, 512], P(('blk', 'rel'))
- item_accum_next: float32 [262144], P(('blk', 'rel'))
- relation_step: float32 [512, 512], replicated
- relation_accum_next: float32 [512], replicated
All inputs are finite; a program needn't handle non-finite values.
Results may differ from a plain program's by a relative error of at most 0.0037.
The roundings to bfloat16 on the way count: a program that leaves them out, or rounds other values in their place, can miss the bound.
Values may be sent and summed in bfloat16 or wider, within the bound.
A program may use at most 64 MiB of HBM per device.

v0:
```python
import jax
import jax.numpy as jnp
from jax import lax
from jax.sharding import PartitionSpec as P

learn_rate = 0.1
epsilon = 1e-06


def from_everyone(shard, axis):
    copies = jnp.broadcast_to(shard, (lax.axis_size(axis), *shard.shape))
    return lax.all_to_all(copies, axis, split_axis=0, concat_axis=0, tiled=True)


def in_order(pieces, dim):
    pieces = jnp.moveaxis(pieces, 0, dim)
    dims = pieces.shape
    return pieces.reshape(*dims[:dim], dims[dim] * dims[dim + 1], *dims[dim + 2 :])


def collect(shard, axis, dim):
    pieces = from_everyone(shard, axis)
    return in_order(pieces, dim)


def in_blocks(shard, dim, peers):
    before, after = (shard.shape[:dim], shard.shape[dim + 1 :])
    return jnp.moveaxis(shard.reshape(*before, peers, -1, *after), dim, 0)


def sum_at_owner(shard, axis, dim):
    peers = lax.axis_size(axis)
    pieces = lax.all_to_all(in_blocks(shard, dim, peers), axis, 0, 0, tiled=True)
    return jnp.sum(pieces, axis=0)


def from_behind(shard, axis, by):
    peers = lax.axis_size(axis)
    return lax.ppermute(shard, axis, [(i, (i + by) % peers) for i in range(peers)])


def adagrad_rows(table, accum, grads):
    accum_next = accum + jnp.mean(grads * grads, axis=1)
    return (table - learn_rate * grads * lax.rsqrt(accum_next + epsilon)[:, None], accum_next)


def per_device(user_table, user_accum, item_table, item_accum, relation, relation_accum, targets):
    blocks = lax.axis_size("blk")
    rounds = targets.shape[0]
    users_now, user_sums = (user_table, user_accum)
    items_now, item_sums = (item_table, item_accum)
    relation_local = jnp.zeros((relation.shape[0], relation.shape[1]), jnp.float32)
    for turn in range(rounds):
        whole_users = collect(users_now.astype(jnp.bfloat16), "rel", 0)
        item_bf = items_now.astype(jnp.bfloat16)
        anchor = jnp.dot(whole_users, relation, preferred_element_type=jnp.float32).astype(
            jnp.bfloat16
        )
        scores = lax.dot_general(
            anchor, item_bf, (((1,), (1,)), ((), ())), preferred_element_type=jnp.float32
        )
        errors = (jax.nn.sigmoid(scores) - targets[turn].astype(jnp.float32)).astype(jnp.bfloat16)
        mapped = lax.dot_general(
            item_bf, relation, (((1,), (1,)), ((), ())), preferred_element_type=jnp.float32
        ).astype(jnp.bfloat16)
        user_grad = sum_at_owner(
            jnp.dot(errors, mapped, preferred_element_type=jnp.float32), "rel", 0
        )
        item_grad = lax.dot_general(
            errors, anchor, (((0,), (0,)), ((), ())), preferred_element_type=jnp.float32
        )
        crossed = lax.dot_general(
            whole_users, errors, (((0,), (0,)), ((), ())), preferred_element_type=jnp.float32
        ).astype(jnp.bfloat16)
        term = jnp.dot(crossed, item_bf, preferred_element_type=jnp.float32)
        relation_local = relation_local + term
        users_now, user_sums = adagrad_rows(users_now, user_sums, user_grad)
        items_now, item_sums = adagrad_rows(items_now, item_sums, item_grad)
        items_now, item_sums = from_behind((items_now, item_sums), "blk", 1)
    total = lax.psum(relation_local, ("blk", "rel"))
    mean_grad = total / (blocks * rounds)
    accum_next = relation_accum + jnp.mean(mean_grad * mean_grad, axis=1)
    relation_step = mean_grad * lax.rsqrt(accum_next + epsilon)[:, None]
    return (users_now, user_sums, items_now, item_sums, relation_step, accum_next)


def solution(mesh):
    return jax.shard_map(
        per_device,
        mesh=mesh,
        in_specs=(
            P(("blk", "rel"), None),
            P(("blk", "rel")),
            P(("blk", "rel"), None),
            P(("blk", "rel")),
            P(),
            P(),
            P(None, "blk", "rel"),
        ),
        out_specs=(
            P(("blk", "rel"), None),
            P(("blk", "rel")),
            P(("blk", "rel"), None),
            P(("blk", "rel")),
            P(),
            P(),
        ),
        check_vma=False,
    )
```

profile of v0, /device:TPU:2, one launch (start us, length us, event | category | flops | bytes accessed | tf_op | source)
XLA Modules:
  0.0 427.7 jit_solution(13035519853064472672)
XLA Ops:
  7.2 0.0 copy-start
  7.2 1.4 convert_element_type.49
  8.5 1.0 broadcast_in_dim.4
  9.6 4.5 %all-to-all-start = ((bf16[2,512,512]{2,1,0:T(8,128)(2,1)}), bf16[2,512,512]{2,1,0:T(8,128)(2,1)}, u32[]{:S(2)}, u32[]{:S(2)}) async-start(bf16[2,512,512]{2,1,0:T(8,128)(2,1)} %broadcast_in_dim.4), calls=%async_computation | async-start | bytes 2097152 | tf_op jit(solution)/shard_map/all_to_all | solution.py:12
  14.0 1.9 copy.13
  16.0 13.5 %all-to-all-done = bf16[2,512,512]{2,1,0:T(8,128)(2,1)} async-done(((bf16[2,512,512]{2,1,0:T(8,128)(2,1)}), bf16[2,512,512]{2,1,0:T(8,128)(2,1)}, u32[]{:S(2)}, u32[]{:S(2)}) %all-to-all-start) | async-done | bytes 1048608 | tf_op jit(solution)/shard_map/all_to_all | solution.py:12
  29.5 0.0 copy-start.2
  29.5 0.0 copy-done
  29.5 2.1 convolution_convert_fusion.5
  31.6 0.0 copy-done.2
  31.6 3.3 fusion.1
  34.9 0.0 copy-start.7
  34.9 1.3 copy-done.7
  36.2 2.7 multiply_reduce_fusion.1
  38.9 5.4 %fusion.2 = f32[1024,512]{1,0:T(8,128)} fusion(bf16[1024,1024]{1,0:T(8,128)(2,1)} %copy-done.7, bf16[512,512]{1,0:T(8,128)(2,1)S(1)} %copy-done, f32[1024,512]{1,0:T(8,128)} %param.9), kind=kOutput, calls=%fused_computation.20 | convolution fusion | flops 1611661312 | bytes 6815744 | tf_op jit(solution)/shard_map/dot_general | solution.py:67
  44.3 0.0 copy-start.4
  44.3 4.9 %all-to-all-start.1 = ((f32[2,512,512]{2,1,0:T(8,128)}), f32[2,512,512]{2,1,0:T(8,128)}, u32[]{:S(2)}, u32[]{:S(2)}) async-start(f32[2,512,512]{2,1,0:T(8,128)} %bitcast.29), calls=%async_computation.1 | async-start | bytes 4194304 | tf_op jit(solution)/shard_map/all_to_all | solution.py:33
  49.2 0.0 copy-done.4
  49.3 3.5 multiply_subtract_fusion.1
  52.8 0.0 copy-start.3
  52.8 0.0 copy-start.1
  52.8 0.0 collective-permute-start
  52.8 44.8 %all-to-all-done.1 = f32[2,512,512]{2,1,0:T(8,128)} async-done(((f32[2,512,512]{2,1,0:T(8,128)}), f32[2,512,512]{2,1,0:T(8,128)}, u32[]{:S(2)}, u32[]{:S(2)}) %all-to-all-start.1) | async-done | bytes 2097184 | tf_op jit(solution)/shard_map/all_to_all | solution.py:33
  97.6 1.9 reduce_sum.63
  99.4 0.1 multiply_reduce_fusion.4
  99.6 0.0 copy-done.3
  99.6 0.0 copy-done.1
  99.6 0.2 fusion.5
  99.8 1.0 broadcast_in_dim.5
  100.8 4.4 %all-to-all-start.2 = ((bf16[2,512,512]{2,1,0:T(8,128)(2,1)}), bf16[2,512,512]{2,1,0:T(8,128)(2,1)}, u32[]{:S(2)}, u32[]{:S(2)}) async-start(bf16[2,512,512]{2,1,0:T(8,128)(2,1)} %broadcast_in_dim.5), calls=%async_computation.2 | async-start | bytes 2097152 | tf_op jit(solution)/shard_map/all_to_all | solution.py:12
  105.3 0.0 all-reduce.2.cloned.1.call-start
  105.3 0.3 collective-permute-start.1
  105.6 5.3 %fusion.4 = f32[512,512]{1,0:T(8,128)} fusion(bf16[1024,1024]{1,0:T(8,128)(2,1)} %copy-done.7, bf16[1024,512]{1,0:T(8,128)(2,1)} %bitcast, f32[1024,512]{1,0:T(8,128)} %param.9), kind=kOutput, calls=%fused_computation.22 | convolution fusion | flops 1611661312 | bytes 6291456 | tf_op jit(solution)/shard_map/dot_general | solution.py:75
  110.9 8.1 %all-to-all-done.2 = bf16[2,512,512]{2,1,0:T(8,128)(2,1)} async-done(((bf16[2,512,512]{2,1,0:T(8,128)(2,1)}), bf16[2,512,512]{2,1,0:T(8,128)(2,1)}, u32[]{:S(2)}, u32[]{:S(2)}) %all-to-all-start.2) | async-done | bytes 1048608 | tf_op jit(solution)/shard_map/all_to_all | solution.py:12
  119.1 1.9 convolution_convert_fusion.3
  121.0 0.0 copy-start.6
  121.0 0.0 collective-permute-done
  121.0 0.9 copy-done.6
  122.0 5.2 %fusion = bf16[1024,1024]{1,0:T(8,128)(2,1)} fusion(bf16[1024,512]{1,0:T(8,128)(2,1)S(1)} %convolution_convert_fusion.3, bf16[2,1024,1024]{2,1,0:T(8,128)(2,1)} %param.13, f32[1024,512]{0,1:T(8,128)} %collective-permute-done), kind=kOutput, calls=%fused_computation.1 | convolution fusion | flops 1080557568 | bytes 7340032 | tf_op jit(solution)/shard_map/dot_general | solution.py:59
  127.2 5.6 %convolution_add_fusion = f32[512,512]{1,0:T(8,128)} fusion(f32[512,512]{1,0:T(8,128)} %fusion.4, bf16[1024,512]{1,0:T(8,128)(2,1)} %bitcast.3, bf16[1024,1024]{1,0:T(8,128)(2,1)} %fusion, f32[1024,512]{0,1:T(8,128)} %collective-permute-done), kind=kOutput, calls=%fused_computation.14 | convolution fusion | flops 1611923456 | bytes 7340032 | tf_op jit(solution)/shard_map/dot_general | solution.py:75
  132.8 4.5 %multiply_reduce_fusion = (f32[1024]{0:T(1024)S(1)}, f32[1024,512]{0,1:T(8,128)}) fusion(bf16[1024,1024]{1,0:T(8,128)(2,1)} %fusion, bf16[1024,512]{1,0:T(8,128)(2,1)} %copy-done.6), kind=kOutput, calls=%fused_computation.5 | convolution fusion | flops 1074789376 | bytes 5246976 | tf_op jit(solution)/shard_map/dot_general | solution.py:69
  137.2 0.0 all-reduce.2.cloned.1.call-update
  137.2 0.0 collective-permute-done.1
  137.3 4.2 multiply_subtract_fusion
  141.4 0.0 collective-permute-start.2
  141.4 5.4 %fusion.3 = f32[1024,512]{1,0:T(8,128)} fusion(bf16[1024,1024]{1,0:T(8,128)(2,1)} %fusion, bf16[512,512]{1,0:T(8,128)(2,1)S(1)} %copy-done, f32[1024,512]{0,1:T(8,128)} %collective-permute-done), kind=kOutput, calls=%fused_computation.21 | convolution fusion | flops 1611661312 | bytes 6815744 | tf_op jit(solution)/shard_map/dot_general | solution.py:67
  146.8 0.0 copy-start.5
  146.8 5.0 %all-to-all-start.3 = ((f32[2,512,512]{2,1,0:T(8,128)}), f32[2,512,512]{2,1,0:T(8,128)}, u32[]{:S(2)}, u32[]{:S(2)}) async-start(f32[2,512,512]{2,1,0:T(8,128)} %bitcast.28), calls=%async_computation.3 | async-start | bytes 4194304 | tf_op jit(solution)/shard_map/all_to_all | solution.py:33
  151.8 0.1 collective-permute-start.3
  151.9 38.7 %collective-permute-done.3 = f32[1024]{0:T(1024)S(1)} collective-permute-done((f32[1024]{0:T(1024)S(1)}, f32[1024]{0:T(1024)S(1)}, u32[]{:S(2)}, u32[]{:S(2)}) %collective-permute-start.3) | collective-permute-done | bytes 4128 | tf_op jit(solution)/shard_map/ppermute | solution.py:39
  190.7 215.1 %all-reduce.2.cloned.1.call-done = f32[512,512]{1,0:T(8,128)} async-done(((f32[512,512]{1,0:T(8,128)}), f32[512,512]{1,0:T(8,128)}) %all-reduce.2.cloned.1.call-update) | async-done | bytes 1048592 | tf_op jit(solution)/shard_map/psum | solution.py:80
  405.8 1.4 multiply_reduce_fusion.2
  407.2 0.0 copy-done.5
  407.2 0.6 rsqrt_multiply_fusion.2
  407.8 2.3 broadcast_multiply_fusion
  410.1 0.0 all-to-all-done.3
  410.1 2.9 reduce_sum.66
  413.0 1.4 multiply_reduce_fusion.3
  414.4 0.6 rsqrt_multiply_fusion.3
  414.9 2.4 multiply_subtract_fusion.2
  417.4 0.0 collective-permute-done.2
  417.4 2.9 copy.14
  420.3 0.6 copy.17
  (3 shorter events, 0.0 us)
Async XLA Ops:
  7.2 22.3 %copy-start = (bf16[512,512]{1,0:T(8,128)(2,1)S(1)}, bf16[512,512]{1,0:T(8,128)(2,1)}, u32[]{:S(2)}) copy-start(bf16[512,512]{1,0:T(8,128)(2,1)} %param.11) | copy-start | bytes 1572868
  9.6 19.9 %all-to-all-start = ((bf16[2,512,512]{2,1,0:T(8,128)(2,1)}), bf16[2,512,512]{2,1,0:T(8,128)(2,1)}, u32[]{:S(2)}, u32[]{:S(2)}) async-start(bf16[2,512,512]{2,1,0:T(8,128)(2,1)} %broadcast_in_dim.4), calls=%async_computation | async-start | bytes 2097152 | tf_op jit(solution)/shard_map/all_to_all | solution.py:12
  29.5 2.1 copy-start.2
  34.9 1.3 copy-start.7
  44.3 5.0 %copy-start.4 = (f32[1024]{0:T(1024)S(1)}, f32[1024]{0:T(1024)}, u32[]{:S(2)}) copy-start(f32[1024]{0:T(1024)} %param.10) | copy-start | bytes 12292
  44.3 53.3 %all-to-all-start.1 = ((f32[2,512,512]{2,1,0:T(8,128)}), f32[2,512,512]{2,1,0:T(8,128)}, u32[]{:S(2)}, u32[]{:S(2)}) async-start(f32[2,512,512]{2,1,0:T(8,128)} %bitcast.29), calls=%async_computation.1 | async-start | bytes 4194304 | tf_op jit(solution)/shard_map/all_to_all | solution.py:33
  52.8 46.8 %copy-start.3 = (f32[512]{0:T(512)S(1)}, f32[512]{0:T(512)}, u32[]{:S(2)}) copy-start(f32[512]{0:T(512)} %param.8) | copy-start | bytes 6148
  52.8 46.8 %copy-start.1 = (f32[512,512]{1,0:T(8,128)S(1)}, f32[512,512]{1,0:T(8,128)}, u32[]{:S(2)}) copy-start(f32[512,512]{1,0:T(8,128)} %param.7) | copy-start | bytes 3145732
  52.8 68.2 %collective-permute-start = (f32[1024,512]{0,1:T(8,128)}, f32[1024,512]{0,1:T(8,128)}, u32[]{:S(2)}, u32[]{:S(2)}) collective-permute-start(f32[1024,512]{0,1:T(8,128)} %multiply_subtract_fusion.1), channel_id=1, source_target_pairs={{0,2},{2,4},{4,6},{6,8},{8,10},{10,12},{12,14},{14,16},{16,18},{18... | collective-permute-start | bytes 6291464 | tf_op jit(solution)/shard_map/ppermute | solution.py:39
  100.8 18.2 %all-to-all-start.2 = ((bf16[2,512,512]{2,1,0:T(8,128)(2,1)}), bf16[2,512,512]{2,1,0:T(8,128)(2,1)}, u32[]{:S(2)}, u32[]{:S(2)}) async-start(bf16[2,512,512]{2,1,0:T(8,128)(2,1)} %broadcast_in_dim.5), calls=%async_computation.2 | async-start | bytes 2097152 | tf_op jit(solution)/shard_map/all_to_all | solution.py:12
  105.3 300.5 %all-reduce.2.cloned.1.call-start = ((), (), s32[]{:S(2)}) async-start(), calls=%async_computation.4 | async-start | bytes 2097152 | tf_op jit(solution)/shard_map/psum | solution.py:80
  105.3 31.9 %collective-permute-start.1 = (f32[1024]{0:T(1024)S(1)}, f32[1024]{0:T(1024)S(1)}, u32[]{:S(2)}, u32[]{:S(2)}) collective-permute-start(f32[1024]{0:T(1024)S(1)} %get-tuple-element.19), channel_id=1, source_target_pairs={{0,2},{2,4},{4,6},{6,8},{8,10},{10,12},{12,14},{14,16},{16,18},{18... | collective-permute-start | bytes 12296 | tf_op jit(solution)/shard_map/ppermute | solution.py:39
  121.0 1.0 copy-start.6
  141.4 275.9 %collective-permute-start.2 = (f32[1024,512]{0,1:T(8,128)}, f32[1024,512]{0,1:T(8,128)}, u32[]{:S(2)}, u32[]{:S(2)}) collective-permute-start(f32[1024,512]{0,1:T(8,128)} %multiply_subtract_fusion), channel_id=1, source_target_pairs={{0,2},{2,4},{4,6},{6,8},{8,10},{10,12},{12,14},{14,16},{16,18},{18... | collective-permute-start | bytes 6291464 | tf_op jit(solution)/shard_map/ppermute | solution.py:39
  146.8 260.4 %copy-start.5 = (f32[512]{0:T(512)S(1)}, f32[512]{0:T(512)}, u32[]{:S(2)}) copy-start(f32[512]{0:T(512)} %param.12) | copy-start | bytes 6148
  146.8 263.3 %all-to-all-start.3 = ((f32[2,512,512]{2,1,0:T(8,128)}), f32[2,512,512]{2,1,0:T(8,128)}, u32[]{:S(2)}, u32[]{:S(2)}) async-start(f32[2,512,512]{2,1,0:T(8,128)} %bitcast.28), calls=%async_computation.3 | async-start | bytes 4194304 | tf_op jit(solution)/shard_map/all_to_all | solution.py:33
  151.8 38.8 %collective-permute-start.3 = (f32[1024]{0:T(1024)S(1)}, f32[1024]{0:T(1024)S(1)}, u32[]{:S(2)}, u32[]{:S(2)}) collective-permute-start(f32[1024]{0:T(1024)S(1)} %get-tuple-element.15), channel_id=1, source_target_pairs={{0,2},{2,4},{4,6},{6,8},{8,10},{10,12},{12,14},{14,16},{16,18},{18... | collective-permute-start | bytes 12296 | tf_op jit(solution)/shard_map/ppermute | solution.py:39
Sparse Core Ops, SparseCore 0:
  137.4 268.3 all-reduce.1
where the time goes:
time: 429 us; the launch traced here: 428 us
  waiting for transfers between devices  320 us (75%)
  matrix products  41.4 us (10%)
  other arithmetic  22.8 us (5%)
  starting transfers between devices  19.2 us (4%)
  between operations  14.2 us (3%)
  local copies, waits for them, and re-layouts  9.78 us (2%)
    psum x1, waiting for transfers between devices, per_device(): total = lax.psum(relation_local, ('blk', 'rel'))  215 us
    all_to_all x2, waiting for transfers between devices, sum_at_owner(): lax.all_to_all(in_blocks(shard, dim, peers), axis, 0, 0, tiled=True)  44.8 us
    ppermute x4, waiting for transfers between devices, from_behind(): lax.ppermute(shard, axis, [(i, (i + by) % peers) for i in range(peers)])  38.8 us
    all_to_all x2, waiting for transfers between devices, from_everyone(): return lax.all_to_all(copies, axis, split_axis=0, concat_axis=0, tiled=True)  21.7 us
    dot_general x2, matrix products, per_device(): term = jnp.dot(crossed, item_bf, preferred_element_type=jnp.float32)  10.9 us
    dot_general x2, matrix products, per_device(): jnp.dot(errors, mapped, preferred_element_type=jnp.float32)  10.8 us
    sub x3, other arithmetic, adagrad_rows(): table - learn_rate * grads * lax.rsqrt(accum_next + epsilon)[:, None]  10.1 us
    all_to_all x2, starting transfers between devices, sum_at_owner(): lax.all_to_all(in_blocks(shard, dim, peers), axis, 0, 0, tiled=True)  9.91 us
  transfers between devices with their start and end apart: 9, of which 5 were waited for; matrix products, arithmetic and copies ran while one was open for 12% of the time, Pallas kernels for 0%

commit v1 on v0

--- a/solution.py
+++ b/solution.py
@@ -77,7 +77,7 @@
         users_now, user_sums = adagrad_rows(users_now, user_sums, user_grad)
         items_now, item_sums = adagrad_rows(items_now, item_sums, item_grad)
         items_now, item_sums = from_behind((items_now, item_sums), "blk", 1)
-    total = lax.psum(relation_local, ("blk", "rel"))
+    total = lax.psum(lax.psum(relation_local, "rel"), "blk")
     mean_grad = total / (blocks * rounds)
     accum_next = relation_accum + jnp.mean(mean_grad * mean_grad, axis=1)
     relation_step = mean_grad * lax.rsqrt(accum_next + epsilon)[:, None]

time: 429 us -> 1330 us (3.10)
  waiting for transfers between devices: 320 us -> 1220 us
    psum x1 -> x2, waiting for transfers between devices: 215 us -> 1150 us  [per_device(): total = lax.psum(lax.psum(relation_local, 'rel'), 'blk')]
    ppermute x4, waiting for transfers between devices: 38.8 us -> 3.03 us  [from_behind(): lax.ppermute(shard, axis, [(i, (i + by) % peers) for i in range(peers)])]
  transfers between devices with their start and end apart: 9 -> 10, of which waited for: 5 -> 6; matrix products, arithmetic and copies ran while one was open for 12% -> 4% of each run, Pallas kernels for 0% -> 0%
where the time goes in v1:
time: 1330 us
  waiting for transfers between devices  1220 us (92%)
  matrix products  41.4 us (3%)
  other arithmetic  22.8 us (2%)
  starting transfers between devices  19.1 us (1%)
  between operations  14.2 us (1%)
    psum x2, waiting for transfers between devices, per_device(): total = lax.psum(lax.psum(relation_local, 'rel'), 'blk')  1150 us
    all_to_all x2, waiting for transfers between devices, sum_at_owner(): lax.all_to_all(in_blocks(shard, dim, peers), axis, 0, 0, tiled=True)  44.8 us
  transfers between devices with their start and end apart: 10, of which 6 were waited for; matrix products, arithmetic and copies ran while one was open for 4% of the time, Pallas kernels for 0%

profile of v1, /device:TPU:2, one launch (start us, length us, event | category | flops | bytes accessed | tf_op | source)
XLA Modules:
  0.0 1325.1 jit_solution(2742707844427058937)
XLA Ops:
  7.2 0.0 copy-start
  7.2 1.4 convert_element_type.49
  8.5 1.0 broadcast_in_dim.4
  9.6 4.5 all-to-all-start
  14.0 1.9 copy.13
  16.0 13.5 %all-to-all-done = bf16[2,512,512]{2,1,0:T(8,128)(2,1)} async-done(((bf16[2,512,512]{2,1,0:T(8,128)(2,1)}), bf16[2,512,512]{2,1,0:T(8,128)(2,1)}, u32[]{:S(2)}, u32[]{:S(2)}) %all-to-all-start) | async-done | bytes 1048608 | tf_op jit(solution)/shard_map/all_to_all | solution.py:12
  29.5 0.0 copy-start.2
  29.5 0.0 copy-done
  29.5 2.1 convolution_convert_fusion.5
  31.6 0.0 copy-done.2
  31.6 3.3 fusion.1
  34.9 0.0 copy-start.7
  34.9 1.3 copy-done.7
  36.2 2.7 multiply_reduce_fusion.1
  38.9 5.4 fusion.2
  44.3 0.0 copy-start.4
  44.3 4.9 all-to-all-start.1
  49.2 0.0 copy-done.4
  49.3 3.5 multiply_subtract_fusion.1
  52.8 0.0 copy-start.3
  52.8 0.0 collective-permute-start
  52.8 44.8 %all-to-all-done.1 = f32[2,512,512]{2,1,0:T(8,128)} async-done(((f32[2,512,512]{2,1,0:T(8,128)}), f32[2,512,512]{2,1,0:T(8,128)}, u32[]{:S(2)}, u32[]{:S(2)}) %all-to-all-start.1) | async-done | bytes 2097184 | tf_op jit(solution)/shard_map/all_to_all | solution.py:33
  97.6 1.9 reduce_sum.63
  99.4 0.1 multiply_reduce_fusion.4
  99.6 0.0 copy-done.3
  99.6 0.0 copy-done.1
  99.6 0.2 fusion.5
  99.8 1.0 broadcast_in_dim.5
  100.8 4.4 all-to-all-start.2
  105.3 0.0 all-reduce.3.cloned.1.call-start
  105.3 0.3 collective-permute-start.1
  105.6 5.3 fusion.4
  110.9 8.1 all-to-all-done.2
  119.1 1.9 convolution_convert_fusion.3
  121.0 0.0 copy-start.6
  121.0 0.0 collective-permute-done
  121.0 0.9 copy-done.6
  122.0 5.2 fusion
  127.2 5.6 convolution_add_fusion
  132.8 4.5 multiply_reduce_fusion
  137.2 0.0 all-reduce.3.cloned.1.call-update
  137.2 0.0 collective-permute-done.1
  137.3 4.2 multiply_subtract_fusion
  141.4 0.0 collective-permute-start.2
  141.4 5.4 fusion.3
  146.8 4.8 all-to-all-start.3
  151.7 0.0 all-reduce.5.cloned.1.call-start
  151.7 64.1 %all-reduce.3.cloned.1.call-done = f32[512,512]{1,0:T(8,128)} async-done(((f32[512,512]{1,0:T(8,128)}), f32[512,512]{1,0:T(8,128)}) %all-reduce.3.cloned.1.call-update) | async-done | bytes 1048592 | tf_op jit(solution)/shard_map/psum | solution.py:80
  215.8 0.0 all-reduce.5.cloned.1.call-update
  215.8 0.1 collective-permute-start.3
  215.9 3.0 collective-permute-done.3
  218.9 0.0 all-to-all-done.3
  218.9 2.9 reduce_sum.66
  221.8 1.4 multiply_reduce_fusion.3
  223.1 0.6 rsqrt_multiply_fusion.3
  223.7 2.4 multiply_subtract_fusion.2
  226.2 0.0 collective-permute-done.2
  226.2 2.9 copy.14
  229.1 1084.3 %all-reduce.5.cloned.1.call-done = f32[512,512]{1,0:T(8,128)} async-done(((f32[512,512]{1,0:T(8,128)}), f32[512,512]{1,0:T(8,128)}) %all-reduce.5.cloned.1.call-update) | async-done | bytes 1048592 | tf_op jit(solution)/shard_map/psum | solution.py:80
  1313.4 1.4 multiply_reduce_fusion.2
  1314.8 0.0 copy-done.5
  1314.8 0.6 rsqrt_multiply_fusion.2
  1315.4 2.3 broadcast_multiply_fusion
  1317.7 0.6 copy.18
  (5 shorter events, 0.0 us)
Async XLA Ops:
  7.2 22.3 %copy-start = (bf16[512,512]{1,0:T(8,128)(2,1)S(1)}, bf16[512,512]{1,0:T(8,128)(2,1)}, u32[]{:S(2)}) copy-start(bf16[512,512]{1,0:T(8,128)(2,1)} %param.11) | copy-start | bytes 1572868
  9.6 19.9 %all-to-all-start = ((bf16[2,512,512]{2,1,0:T(8,128)(2,1)}), bf16[2,512,512]{2,1,0:T(8,128)(2,1)}, u32[]{:S(2)}, u32[]{:S(2)}) async-start(bf16[2,512,512]{2,1,0:T(8,128)(2,1)} %broadcast_in_dim.4), calls=%async_computation | async-start | bytes 2097152 | tf_op jit(solution)/shard_map/all_to_all | solution.py:12
  29.5 2.1 copy-start.2
  34.9 1.3 copy-start.7
  44.3 5.0 copy-start.4
  44.3 53.3 %all-to-all-start.1 = ((f32[2,512,512]{2,1,0:T(8,128)}), f32[2,512,512]{2,1,0:T(8,128)}, u32[]{:S(2)}, u32[]{:S(2)}) async-start(f32[2,512,512]{2,1,0:T(8,128)} %bitcast.29), calls=%async_computation.1 | async-start | bytes 4194304 | tf_op jit(solution)/shard_map/all_to_all | solution.py:33
  52.8 46.8 %copy-start.3 = (f32[512]{0:T(512)S(1)}, f32[512]{0:T(512)}, u32[]{:S(2)}) copy-start(f32[512]{0:T(512)} %param.8) | copy-start | bytes 6148
  52.8 46.8 %copy-start.1 = (f32[512,512]{1,0:T(8,128)S(1)}, f32[512,512]{1,0:T(8,128)}, u32[]{:S(2)}) copy-start(f32[512,512]{1,0:T(8,128)} %param.7) | copy-start | bytes 3145732
  52.8 68.2 %collective-permute-start = (f32[1024,512]{0,1:T(8,128)}, f32[1024,512]{0,1:T(8,128)}, u32[]{:S(2)}, u32[]{:S(2)}) collective-permute-start(f32[1024,512]{0,1:T(8,128)} %multiply_subtract_fusion.1), channel_id=1, source_target_pairs={{0,2},{2,4},{4,6},{6,8},{8,10},{10,12},{12,14},{14,16},{16,18},{18... | collective-permute-start | bytes 6291464 | tf_op jit(solution)/shard_map/ppermute | solution.py:39
  100.8 18.2 %all-to-all-start.2 = ((bf16[2,512,512]{2,1,0:T(8,128)(2,1)}), bf16[2,512,512]{2,1,0:T(8,128)(2,1)}, u32[]{:S(2)}, u32[]{:S(2)}) async-start(bf16[2,512,512]{2,1,0:T(8,128)(2,1)} %broadcast_in_dim.5), calls=%async_computation.2 | async-start | bytes 2097152 | tf_op jit(solution)/shard_map/all_to_all | solution.py:12
  105.3 110.5 %all-reduce.3.cloned.1.call-start = ((), (), s32[]{:S(2)}) async-start(), calls=%async_computation.4 | async-start | bytes 2097152 | tf_op jit(solution)/shard_map/psum | solution.py:80
  105.3 31.9 %collective-permute-start.1 = (f32[1024]{0:T(1024)S(1)}, f32[1024]{0:T(1024)S(1)}, u32[]{:S(2)}, u32[]{:S(2)}) collective-permute-start(f32[1024]{0:T(1024)S(1)} %get-tuple-element.19), channel_id=1, source_target_pairs={{0,2},{2,4},{4,6},{6,8},{8,10},{10,12},{12,14},{14,16},{16,18},{18... | collective-permute-start | bytes 12296 | tf_op jit(solution)/shard_map/ppermute | solution.py:39
  121.0 1.0 copy-start.6
  141.4 84.7 %collective-permute-start.2 = (f32[1024,512]{0,1:T(8,128)}, f32[1024,512]{0,1:T(8,128)}, u32[]{:S(2)}, u32[]{:S(2)}) collective-permute-start(f32[1024,512]{0,1:T(8,128)} %multiply_subtract_fusion), channel_id=1, source_target_pairs={{0,2},{2,4},{4,6},{6,8},{8,10},{10,12},{12,14},{14,16},{16,18},{18... | collective-permute-start | bytes 6291464 | tf_op jit(solution)/shard_map/ppermute | solution.py:39
  146.8 72.1 %all-to-all-start.3 = ((f32[2,512,512]{2,1,0:T(8,128)}), f32[2,512,512]{2,1,0:T(8,128)}, u32[]{:S(2)}, u32[]{:S(2)}) async-start(f32[2,512,512]{2,1,0:T(8,128)} %bitcast.28), calls=%async_computation.3 | async-start | bytes 4194304 | tf_op jit(solution)/shard_map/all_to_all | solution.py:33
  151.7 1161.7 %all-reduce.5.cloned.1.call-start = ((), (), s32[]{:S(2)}) async-start(), calls=%async_computation.5 | async-start | bytes 2097152 | tf_op jit(solution)/shard_map/psum | solution.py:80
  215.8 3.1 collective-permute-start.3
  226.2 1088.6 %copy-start.5 = (f32[512]{0:T(512)S(1)}, f32[512]{0:T(512)}, u32[]{:S(2)}) copy-start(f32[512]{0:T(512)} %param.12) | copy-start | bytes 6148
Sparse Core Ops, SparseCore 0:
  137.4 78.3 all-reduce.2
  218.4 1094.9 all-reduce.4
